TPU v7x, 32 devices: a whole 2x2x4 slice. The times are simulated.
32 devices in a mesh: dp: 8 (over z, x), tensor: 4 (over y, core).
Axes of the slice: x: 2, y: 2, z: 4, core: 2. Of those that a mesh axis runs over, the one named last changes fastest.
Arguments:
- tokens: bfloat16 [8, 256, 4096], P('dp', 'tensor'), may hold values from -6 to 6
- gain: bfloat16 [4096], replicated, may hold values from 0.5 to 1.5
- wq: bfloat16 [4096, 4096], P(None, 'tensor'), may hold values from -0.09375 to 0.09375
- bq: bfloat16 [4096], P('tensor'), may hold values from -5 to 5
- wkv: bfloat16 [4096, 1024], P(None, 'tensor'), may hold values from -0.09375 to 0.09375
- bkv: bfloat16 [1024], P('tensor'), may hold values from -5 to 5
- wo: bfloat16 [4096, 4096], P('tensor'), may hold values from -0.375 to 0.375
- check_weights: float32 [8, 256], P('dp'), may hold values from -12 to 12
Outputs:
- attended: bfloat16 [8, 256, 4096], P('dp', 'tensor')
- checksum: float32 [4096], replicated
All inputs are finite; a program needn't handle non-finite values.
Results may differ from a plain program's by a relative error of at most 0.018.
Values may be sent and summed in bfloat16 or wider, within the bound.
A program may use at most 64 MiB of HBM per device.

v0:
```python
import jax
import jax.numpy as jnp
from jax import lax
from jax.sharding import PartitionSpec as P

HEADS = 32
KV = 4
HD = 128
EPS = 1e-06
THETA = 1000000.0


def rope(values, head_size):
    rows = values.shape[0]
    half = head_size // 2
    inverse = THETA ** (-(jnp.arange(half, dtype=jnp.float32) * 2.0 / head_size))
    angles = jnp.arange(rows, dtype=jnp.float32)[:, None] * inverse[None, :]
    cosine = jnp.cos(angles)[:, None, :]
    sine = jnp.sin(angles)[:, None, :]
    shaped = values.reshape(rows, -1, head_size)
    first = shaped[..., :half]
    second = shaped[..., half:]
    turned = jnp.concatenate(
        [first * cosine - second * sine, second * cosine + first * sine], axis=-1
    )
    return turned.reshape(rows, -1)


def local(tokens, gain, wq, bq, wkv, bkv, wo, check_weights):
    states = tokens[0].astype(jnp.float32)
    normed = (
        states
        * lax.rsqrt(jnp.mean(states * states, axis=-1, keepdims=True) + EPS)
        * gain.astype(jnp.float32)
    ).astype(jnp.bfloat16)
    position = lax.axis_index("tensor")
    head_dev = wq.shape[1] // HD
    query_cols = head_dev * HD
    shared = position * head_dev // (HEADS // KV)
    joined_w = jnp.concatenate([wq, wkv], axis=1)
    joined_b = jnp.concatenate([bq, bkv], axis=0).astype(jnp.float32)
    projected = (
        jnp.dot(
            lax.all_gather(normed, "tensor", axis=0, tiled=True),
            joined_w,
            preferred_element_type=jnp.float32,
        )
        + joined_b[None, :]
    )
    seq_rows = projected.shape[0]
    query = rope(projected[:, :query_cols], HD).astype(jnp.bfloat16)
    kv_local = projected[:, query_cols:].astype(jnp.bfloat16)
    kv_whole = lax.all_gather(kv_local, "tensor", axis=1, tiled=True)
    key_part = lax.dynamic_slice_in_dim(kv_whole, shared * HD, HD, 1)
    values = lax.dynamic_slice_in_dim(kv_whole, KV * HD + shared * HD, HD, 1)
    keys = rope(key_part.astype(jnp.float32), HD).astype(jnp.bfloat16)
    scale = HD ** (-0.5)
    block = min(512, seq_rows)
    query_heads = query.reshape(seq_rows, head_dev, HD)
    pieces = []
    for number in range(seq_rows // block):
        stop = (number + 1) * block
        query_block = query_heads[number * block : stop]
        scores = (
            jnp.einsum("qhd,kd->hqk", query_block, keys[:stop], preferred_element_type=jnp.float32)
            * scale
        )
        allowed = jnp.arange(block)[:, None] + number * block >= jnp.arange(stop)[None, :]
        scores = jnp.where(allowed[None, :, :], scores, -1e30)
        probs = jax.nn.softmax(scores, axis=-1).astype(jnp.bfloat16)
        mixed = jnp.einsum(
            "hqk,kd->qhd", probs, values[:stop], preferred_element_type=jnp.float32
        ).astype(jnp.bfloat16)
        pieces.append(mixed.reshape(block, query_cols))
    context = jnp.concatenate(pieces, axis=0)
    summed = lax.psum_scatter(
        jnp.dot(context, wo, preferred_element_type=jnp.float32).astype(jnp.bfloat16),
        "tensor",
        scatter_dimension=0,
        tiled=True,
    )
    attended = summed[None, :, :]
    summary = jnp.dot(
        check_weights[0], context.astype(jnp.float32), precision=lax.Precision.HIGHEST
    )
    term = jnp.dot(summary, wo.astype(jnp.float32), precision=lax.Precision.HIGHEST)
    total = lax.psum(term, ("dp", "tensor"))
    checksum = total / jnp.sqrt(jnp.float32(seq_rows * lax.axis_size("dp")))
    return (attended, checksum)


def solution(mesh):
    placed = (
        P("dp", "tensor", None),
        P(),
        P(None, "tensor"),
        P("tensor"),
        P(None, "tensor"),
        P("tensor"),
        P("tensor", None),
        P("dp", None),
    )
    return jax.shard_map(
        local, mesh=mesh, in_specs=placed, out_specs=(P("dp", "tensor", None), P()), check_vma=False
    )
```

profile of v0, /device:TPU:0, one launch (start us, length us, event | category | flops | bytes accessed | tf_op | source)
XLA Modules:
  0.0 118.1 jit_solution(9520385289400516932)
XLA Ops:
  7.2 0.0 copy-start
  7.2 0.0 copy-start.1
  7.2 0.0 copy-start.2
  7.2 0.0 copy-start.3
  7.2 0.0 all-gather.2.cloned.1.call-start
  7.3 0.8 convert_element_type.43
  8.1 1.2 %fusion.9 = f32[64]{0:T(128)S(1)} fusion(bf16[1,64,4096]{2,1,0:T(8,128)(2,1)} %param.8), kind=kLoop, calls=%fused_computation.15 | loop fusion | flops 786368 | bytes 524544 | tf_op jit(solution)/shard_map/reduce_sum | solution.py:33
  9.4 2.0 %fusion.11 = bf16[64,4096]{1,0:T(8,128)(2,1)} fusion(bf16[1,64,4096]{2,1,0:T(8,128)(2,1)} %param.8, f32[4096]{0:T(1024)S(1)} %convert_element_type.43, f32[64]{0:T(128)S(1)} %add_rsqrt_fusion), kind=kLoop, calls=%fused_computation.17 | loop fusion | flops 1048576 | bytes 1065216 | tf_op jit(solution)/shard_map/convert_element_type | solution.py:35
  11.4 0.0 all-gather.2.cloned.1.call-update
  11.4 0.0 reduce-scatter.2.cloned.1.call-start
  11.5 0.0 copy-done.1
  11.5 0.0 copy-done.2
  11.6 0.5 fusion.24
  12.1 24.8 %all-gather.2.cloned.1.call-done = bf16[256,4096]{1,0:T(8,128)(2,1)} async-done(((bf16[64,4096]{1,0:T(8,128)(2,1)}), bf16[256,4096]{1,0:T(8,128)(2,1)}) %all-gather.2.cloned.1.call-update) | async-done | bytes 2097168 | tf_op jit(solution)/shard_map/all_gather | solution.py:44
  36.9 0.0 copy-done.3
  36.9 7.5 %fusion.5 = f32[256,1280]{1,0:T(8,128)S(1)} fusion(bf16[256,4096]{1,0:T(8,128)(2,1)} %all-gather.2.cloned.1.call-done, bf16[4096,256]{1,0:T(8,128)(2,1)S(1)} %copy-done.3, bf16[4096,1024]{1,0:T(8,128)(2,1)} %param.10, f32[1280]{0:T(1024)S(1)} %maximum_convert_fusion), kind=kOutput, calls=%fused_computation.6 | convolution fusion | flops 2705653760 | bytes 13898752 | tf_op jit(solution)/shard_map/dot_general | solution.py:43
  44.4 0.1 slice_bitcast_fusion
  44.5 7.2 %all_gather.7 = bf16[256,1024]{1,0:T(8,128)(2,1)S(1)} all-gather(bf16[256,256]{1,0:T(8,128)(2,1)S(1)} %slice.37), channel_id=1, replica_groups=mesh['dp'=8,'tensor'=4] {'tensor'}, dimensions={1}, use_global_device_ids=true | all-gather | bytes 655360 | tf_op jit(solution)/shard_map/all_gather | solution.py:53
  51.7 0.5 subtract_convert_fusion.1
  52.3 0.2 copy.19
  52.5 0.3 fusion.39
  52.8 0.4 subtract_convert_fusion
  53.2 2.4 %fusion.40 = (f32[8,256]{1,0:T(8,128)S(1)}, f32[8,256,256]{1,2,0:T(8,128)}) fusion(pred[256,256]{0,1:T(8,128)(4,1)S(1)} %iota_compare_fusion, bf16[256,8,64]{2,0,1:T(8,128)(2,1)S(1)} %get-tuple-element.3, bf16[256,8,64]{2,0,1:T(8,128)(2,1)S(1)} %get-tuple-element.2, bf16[256,1,64]{2,0,1:T(8,128)(2,1)S(1)} %get-tuple-element.7, ...), kind=kOutput, calls=%fused_computation.54 | convolution fusion | flops 137494784 | bytes 2760704 | tf_op jit(solution)/shard_map/sub | solution.py:70
  55.6 1.9 %convolution_convert_fusion.1 = bf16[128,8,256]{2,0,1:T(8,128)(2,1)S(1)} fusion(f32[8,256,256]{1,2,0:T(8,128)} %get-tuple-element.11, f32[8,256]{1,0:T(8,128)S(1)} %get-tuple-element.10, bf16[256,1024]{1,0:T(8,128)(2,1)S(1)} %all_gather.7, s32[]{:T(128)S(6)} %select_n.16), kind=kOutput, calls=%fused_computation.13 | convolution fusion | flops 135528448 | bytes 2695172 | tf_op jit(solution)/shard_map/hqk,kd->qhd/dot_general | solution.py:71
  57.5 7.1 %convolution_convert_fusion = bf16[256,4096]{1,0:T(8,128)(2,1)} fusion(bf16[256,1024]{0,1:T(8,128)(2,1)S(1)} %bitcast.49, bf16[1024,4096]{1,0:T(8,128)(2,1)} %param.14), kind=kOutput, calls=%fused_computation.5 | convolution fusion | flops 2148532224 | bytes 11010048 | tf_op jit(solution)/shard_map/dot_general | solution.py:77
  64.6 0.0 reduce-scatter.2.cloned.1.call-update
  64.7 0.0 copy-done
  64.7 0.5 convolution_bitcast_fusion
  65.2 5.7 %fusion.43 = f32[1,4096]{1,0:T(1,128)S(1)} fusion(f32[1024,1]{0,1:T(1,128)S(1)} %convolution_bitcast_fusion, bf16[1024,4096]{1,0:T(8,128)(2,1)} %param.14), kind=kOutput, calls=%fused_computation.55 | convolution fusion | flops 50331648 | bytes 8409088 | tf_op jit(solution)/shard_map/dot_general | solution.py:86
  70.9 39.7 %psum.7 = f32[4096]{0:T(1024)S(1)} all-reduce(f32[4096]{0:T(1024)S(1)} %bitcast.51), channel_id=1, replica_groups=mesh['dp'=8,'tensor'=4] {'dp','tensor'}, use_global_device_ids=true, to_apply=%region_4.5 | all-reduce | flops 4096 | bytes 32768 | tf_op jit(solution)/shard_map/psum | solution.py:87
  110.6 0.6 broadcast_multiply_fusion
  111.2 0.0 reduce-scatter.2.cloned.1.call-done
  (6 shorter events, 0.1 us)
Async XLA Ops:
  7.2 57.5 %copy-start = (f32[1,256]{1,0:T(1,128)S(1)}, f32[1,256]{1,0:T(1,128)}, u32[]{:S(2)}) copy-start(f32[1,256]{1,0:T(1,128)} %param.15) | copy-start | bytes 3076
  7.2 4.3 %copy-start.1 = (bf16[1024]{0:T(1024)(128)(2,1)S(1)}, bf16[1024]{0:T(1024)(128)(2,1)}, u32[]{:S(2)}) copy-start(bf16[1024]{0:T(1024)(128)(2,1)} %param.11) | copy-start | bytes 6148
  7.2 4.3 %copy-start.2 = (bf16[256]{0:T(256)(128)(2,1)S(1)}, bf16[256]{0:T(256)(128)(2,1)}, u32[]{:S(2)}) copy-start(bf16[256]{0:T(256)(128)(2,1)} %param.13) | copy-start | bytes 1540
  7.2 29.7 %copy-start.3 = (bf16[4096,256]{1,0:T(8,128)(2,1)S(1)}, bf16[4096,256]{1,0:T(8,128)(2,1)}, u32[]{:S(2)}) copy-start(bf16[4096,256]{1,0:T(8,128)(2,1)} %param.12) | copy-start | bytes 6291460
  7.2 29.7 %all-gather.2.cloned.1.call-start = ((), (), s32[]{:S(2)}) async-start(), calls=%async_computation.1 | async-start | bytes 2621440 | tf_op jit(solution)/shard_map/all_gather | solution.py:44
  11.4 99.8 %reduce-scatter.2.cloned.1.call-start = ((), (), s32[]{:S(2)}) async-start(), calls=%async_computation.2 | async-start | bytes 2621440 | tf_op jit(solution)/shard_map/reduce_scatter | solution.py:76
Sparse Core Ops, SparseCore 0:
  11.5 25.2 all-gather.1
  64.8 31.3 reduce-scatter.1
where the time goes:
time: 118 us
  blocking collectives  46.9 us (40%)
  matrix products  25.1 us (21%)
  waiting for transfers between devices  24.8 us (21%)
  between operations  14.2 us (12%)
  other arithmetic  6.25 us (5%)
    psum x1, blocking collectives, local(): total = lax.psum(term, ('dp', 'tensor'))  39.7 us
    all_gather x1, waiting for transfers between devices, local(): lax.all_gather(normed, 'tensor', axis=0, tiled=True)  24.8 us
    dot_general x1, matrix products, local(): jnp.dot(lax.all_gather(normed, 'tensor', axis=0, tiled=True), joined_w, p...  7.53 us
    all_gather x1, blocking collectives, local(): kv_whole = lax.all_gather(kv_local, 'tensor', axis=1, tiled=True)  7.16 us
    dot_general x1, matrix products, local(): jnp.dot(context, wo, preferred_element_type=jnp.float32)  7.11 us
    dot_general x1, matrix products, local(): jnp.dot(summary, wo.astype(jnp.float32), precision=lax.Precision.HIGHEST)  5.68 us
  transfers between devices with their start and end apart: 2, of which 1 were waited for; matrix products, arithmetic and copies ran while one was open for 6% of the time, Pallas kernels for 0%

commit v1 on v0

--- a/solution.py
+++ b/solution.py
@@ -50,7 +50,14 @@
     seq_rows = projected.shape[0]
     query = rope(projected[:, :query_cols], HD).astype(jnp.bfloat16)
     kv_local = projected[:, query_cols:].astype(jnp.bfloat16)
-    kv_whole = lax.all_gather(kv_local, "tensor", axis=1, tiled=True)
+    ring = [kv_local]
+    for hop in range(3):
+        ring.append(lax.ppermute(ring[-1], "tensor", [(dev, (dev + 1) % 4) for dev in range(4)]))
+    kv_whole = jnp.roll(
+        jnp.concatenate(ring[::-1], axis=1),
+        (lax.axis_index("tensor") + 1) * ring[0].shape[1],
+        axis=1,
+    )
     key_part = lax.dynamic_slice_in_dim(kv_whole, shared * HD, HD, 1)
     values = lax.dynamic_slice_in_dim(kv_whole, KV * HD + shared * HD, HD, 1)
     keys = rope(key_part.astype(jnp.float32), HD).astype(jnp.bfloat16)

time: 118 us -> 124 us (1.051)
  waiting for transfers between devices: 24.8 us -> 36.7 us
  blocking collectives: 46.9 us -> 39.8 us
    ppermute x0 -> x3, waiting for transfers between devices: none -> 11.9 us  [local(): lax.ppermute(ring[-1], 'tensor', [(dev, (dev + 1) % 4) for dev in range(4)])]
    all_gather x1 -> x0, blocking collectives: 7.16 us -> none  [local(): kv_whole = lax.all_gather(kv_local, 'tensor', axis=1, tiled=True)]
  transfers between devices with their start and end apart: 2 -> 5, of which waited for: 1 -> 4; matrix products, arithmetic and copies ran while one was open for 6% -> 7% of each run, Pallas kernels for 0% -> 0%
where the time goes in v1:
time: 124 us; the launch traced here: 123 us
  blocking collectives  39.8 us (32%)
  waiting for transfers between devices  36.7 us (30%)
  matrix products  25.2 us (20%)
  between operations  14.3 us (12%)
  other arithmetic  6.33 us (5%)
    psum x1, blocking collectives, local(): total = lax.psum(term, ('dp', 'tensor'))  39.8 us
    all_gather x1, waiting for transfers between devices, local(): lax.all_gather(normed, 'tensor', axis=0, tiled=True)  24.8 us
    ppermute x3, waiting for transfers between devices, local(): lax.ppermute(ring[-1], 'tensor', [(dev, (dev + 1) % 4) for dev in range(4)])  11.9 us
    dot_general x1, matrix products, local(): jnp.dot(lax.all_gather(normed, 'tensor', axis=0, tiled=True), joined_w, p...  7.53 us
    dot_general x1, matrix products, local(): jnp.dot(context, wo, preferred_element_type=jnp.float32)  7.1 us
    dot_general x1, matrix products, local(): jnp.dot(summary, wo.astype(jnp.float32), precision=lax.Precision.HIGHEST)  5.68 us
  transfers between devices with their start and end apart: 5, of which 4 were waited for; matrix products, arithmetic and copies ran while one was open for 7% of the time, Pallas kernels for 0%

profile of v1, /device:TPU:0, one launch (start us, length us, event | category | flops | bytes accessed | tf_op | source)
XLA Modules:
  0.0 123.4 jit_solution(10739767924785312487)
XLA Ops:
  7.2 0.0 copy-start
  7.2 0.0 copy-start.1
  7.2 0.0 copy-start.2
  7.2 0.0 all-gather.2.cloned.1.call-start
  7.3 0.8 convert_element_type.43
  8.1 1.2 %fusion.9 = f32[64]{0:T(128)S(1)} fusion(bf16[1,64,4096]{2,1,0:T(8,128)(2,1)} %param.8), kind=kLoop, calls=%fused_computation.15 | loop fusion | flops 786368 | bytes 524544 | tf_op jit(solution)/shard_map/reduce_sum | solution.py:33
  9.4 2.0 %fusion.11 = bf16[64,4096]{1,0:T(8,128)(2,1)} fusion(bf16[1,64,4096]{2,1,0:T(8,128)(2,1)} %param.8, f32[4096]{0:T(1024)S(1)} %convert_element_type.43, f32[64]{0:T(128)S(1)} %add_rsqrt_fusion), kind=kLoop, calls=%fused_computation.17 | loop fusion | flops 1048576 | bytes 1065216 | tf_op jit(solution)/shard_map/convert_element_type | solution.py:35
  11.4 0.0 all-gather.2.cloned.1.call-update
  11.4 0.0 reduce-scatter.2.cloned.1.call-start
  11.6 0.5 fusion.24
  12.1 24.8 %all-gather.2.cloned.1.call-done = bf16[256,4096]{1,0:T(8,128)(2,1)} async-done(((bf16[64,4096]{1,0:T(8,128)(2,1)}), bf16[256,4096]{1,0:T(8,128)(2,1)}) %all-gather.2.cloned.1.call-update) | async-done | bytes 2097168 | tf_op jit(solution)/shard_map/all_gather | solution.py:44
  36.9 7.5 %fusion.5 = f32[256,1280]{1,0:T(8,128)S(1)} fusion(bf16[256,4096]{1,0:T(8,128)(2,1)} %all-gather.2.cloned.1.call-done, bf16[4096,256]{1,0:T(8,128)(2,1)S(1)} %copy-done.3, bf16[4096,1024]{1,0:T(8,128)(2,1)} %param.10, f32[1280]{0:T(1024)S(1)} %maximum_convert_fusion), kind=kOutput, calls=%fused_computation.6 | convolution fusion | flops 2705653760 | bytes 13898752 | tf_op jit(solution)/shard_map/dot_general | solution.py:43
  44.4 0.3 collective-permute-start
  44.7 0.1 slice_bitcast_fusion
  44.8 0.2 copy.19
  45.0 3.8 %collective-permute-done = bf16[256,256]{1,0:T(8,128)(2,1)S(1)} collective-permute-done((bf16[256,256]{1,0:T(8,128)(2,1)S(1)}, bf16[256,256]{1,0:T(8,128)(2,1)S(1)}, u32[]{:S(2)}, u32[]{:S(2)}) %collective-permute-start) | collective-permute-done | bytes 131104 | tf_op jit(solution)/shard_map/ppermute | solution.py:55
  48.9 0.0 collective-permute-start.1
  48.9 0.3 fusion.39
  49.2 4.1 %collective-permute-done.1 = bf16[256,256]{1,0:T(8,128)(2,1)S(1)} collective-permute-done((bf16[256,256]{1,0:T(8,128)(2,1)S(1)}, bf16[256,256]{1,0:T(8,128)(2,1)S(1)}, u32[]{:S(2)}, u32[]{:S(2)}) %collective-permute-start.1) | collective-permute-done | bytes 131104 | tf_op jit(solution)/shard_map/ppermute | solution.py:55
  53.3 0.0 collective-permute-start.2
  53.3 0.4 subtract_convert_fusion
  53.7 4.0 %collective-permute-done.2 = bf16[256,256]{1,0:T(8,128)(2,1)S(1)} collective-permute-done((bf16[256,256]{1,0:T(8,128)(2,1)S(1)}, bf16[256,256]{1,0:T(8,128)(2,1)S(1)}, u32[]{:S(2)}, u32[]{:S(2)}) %collective-permute-start.2) | collective-permute-done | bytes 131104 | tf_op jit(solution)/shard_map/ppermute | solution.py:55
  57.8 0.1 bitcast_convert_fusion
  57.9 0.5 subtract_convert_fusion.1
  58.5 2.3 %fusion.40 = (f32[8,256]{1,0:T(8,128)S(1)}, f32[8,256,256]{1,2,0:T(8,128)}) fusion(pred[256,256]{0,1:T(8,128)(4,1)S(1)} %iota_compare_fusion, bf16[256,8,64]{2,0,1:T(8,128)(2,1)S(1)} %get-tuple-element.3, bf16[256,8,64]{2,0,1:T(8,128)(2,1)S(1)} %get-tuple-element.2, bf16[256,1,64]{2,0,1:T(8,128)(2,1)S(1)} %get-tuple-element.7, ...), kind=kOutput, calls=%fused_computation.62 | convolution fusion | flops 137494784 | bytes 2760704 | tf_op jit(solution)/shard_map/sub | solution.py:77
  60.8 2.0 %convolution_convert_fusion.1 = bf16[128,8,256]{2,0,1:T(8,128)(2,1)S(1)} fusion(f32[8,256,256]{1,2,0:T(8,128)} %get-tuple-element.11, f32[8,256]{1,0:T(8,128)S(1)} %get-tuple-element.10, bf16[256,2048]{1,0:T(8,128)(2,1)S(1)} %constant_dynamic-update-slice_fusion, s32[]{:T(128)S(6)} %dynamic_slice.14), kind=kOutput, calls=%fused_computation.13 | convolution fusion | flops 135528448 | bytes 2695172 | tf_op jit(solution)/shard_map/hqk,kd->qhd/dot_general | solution.py:78
  62.8 7.1 %convolution_convert_fusion = bf16[256,4096]{1,0:T(8,128)(2,1)} fusion(bf16[256,1024]{0,1:T(8,128)(2,1)S(1)} %bitcast.49, bf16[1024,4096]{1,0:T(8,128)(2,1)} %param.14), kind=kOutput, calls=%fused_computation.5 | convolution fusion | flops 2148532224 | bytes 11010048 | tf_op jit(solution)/shard_map/dot_general | solution.py:84
  69.9 0.0 reduce-scatter.2.cloned.1.call-update
  69.9 0.5 convolution_bitcast_fusion
  70.5 5.7 %fusion.43 = f32[1,4096]{1,0:T(1,128)S(1)} fusion(f32[1024,1]{0,1:T(1,128)S(1)} %convolution_bitcast_fusion, bf16[1024,4096]{1,0:T(8,128)(2,1)} %param.14), kind=kOutput, calls=%fused_computation.63 | convolution fusion | flops 50331648 | bytes 8409088 | tf_op jit(solution)/shard_map/dot_general | solution.py:93
  76.1 39.8 %psum.7 = f32[4096]{0:T(1024)S(1)} all-reduce(f32[4096]{0:T(1024)S(1)} %bitcast.51), channel_id=1, replica_groups=mesh['dp'=8,'tensor'=4] {'dp','tensor'}, use_global_device_ids=true, to_apply=%region_4.5 | all-reduce | flops 4096 | bytes 32768 | tf_op jit(solution)/shard_map/psum | solution.py:94
  115.9 0.6 broadcast_multiply_fusion
  (19 shorter events, 0.2 us)
Async XLA Ops:
  7.2 62.8 %copy-start = (f32[1,256]{1,0:T(1,128)S(1)}, f32[1,256]{1,0:T(1,128)}, u32[]{:S(2)}) copy-start(f32[1,256]{1,0:T(1,128)} %param.15) | copy-start | bytes 3076
  7.2 4.3 %copy-start.1 = (bf16[1024]{0:T(1024)(128)(2,1)S(1)}, bf16[1024]{0:T(1024)(128)(2,1)}, u32[]{:S(2)}) copy-start(bf16[1024]{0:T(1024)(128)(2,1)} %param.11) | copy-start | bytes 6148
  7.2 4.3 %copy-start.2 = (bf16[256]{0:T(256)(128)(2,1)S(1)}, bf16[256]{0:T(256)(128)(2,1)}, u32[]{:S(2)}) copy-start(bf16[256]{0:T(256)(128)(2,1)} %param.13) | copy-start | bytes 1540
  7.2 29.7 %copy-start.3 = (bf16[4096,256]{1,0:T(8,128)(2,1)S(1)}, bf16[4096,256]{1,0:T(8,128)(2,1)}, u32[]{:S(2)}) copy-start(bf16[4096,256]{1,0:T(8,128)(2,1)} %param.12) | copy-start | bytes 6291460
  7.2 29.7 %all-gather.2.cloned.1.call-start = ((), (), s32[]{:S(2)}) async-start(), calls=%async_computation.1 | async-start | bytes 2621440 | tf_op jit(solution)/shard_map/all_gather | solution.py:44
  11.4 105.1 %reduce-scatter.2.cloned.1.call-start = ((), (), s32[]{:S(2)}) async-start(), calls=%async_computation.2 | async-start | bytes 2621440 | tf_op jit(solution)/shard_map/reduce_scatter | solution.py:83
  44.4 4.4 %collective-permute-start = (bf16[256,256]{1,0:T(8,128)(2,1)S(1)}, bf16[256,256]{1,0:T(8,128)(2,1)S(1)}, u32[]{:S(2)}, u32[]{:S(2)}) collective-permute-start(bf16[256,256]{1,0:T(8,128)(2,1)S(1)} %slice.37), channel_id=1, source_target_pairs={{0,1},{1,2},{2,3},{3,0},{4,5},{5,6},{6,7},{7,4},{8,9},{9,10},{10,1... | collective-permute-start | bytes 393224 | tf_op jit(solution)/shard_map/ppermute | solution.py:55
  48.9 4.4 %collective-permute-start.1 = (bf16[256,256]{1,0:T(8,128)(2,1)S(1)}, bf16[256,256]{1,0:T(8,128)(2,1)S(1)}, u32[]{:S(2)}, u32[]{:S(2)}) collective-permute-start(bf16[256,256]{1,0:T(8,128)(2,1)S(1)} %collective-permute-done), channel_id=1, source_target_pairs={{0,1},{1,2},{2,3},{3,0},{4,5},{5,6},{6,7},{7,4},{8,9},{9,10},{10,1... | collective-permute-start | bytes 393224 | tf_op jit(solution)/shard_map/ppermute | solution.py:55
  53.3 4.4 %collective-permute-start.2 = (bf16[256,256]{1,0:T(8,128)(2,1)S(1)}, bf16[256,256]{1,0:T(8,128)(2,1)S(1)}, u32[]{:S(2)}, u32[]{:S(2)}) collective-permute-start(bf16[256,256]{1,0:T(8,128)(2,1)S(1)} %collective-permute-done.1), channel_id=1, source_target_pairs={{0,1},{1,2},{2,3},{3,0},{4,5},{5,6},{6,7},{7,4},{8,9},{9,10},{10,1... | collective-permute-start | bytes 393224 | tf_op jit(solution)/shard_map/ppermute | solution.py:55
Sparse Core Ops, SparseCore 0:
  11.5 25.2 all-gather.1
  70.1 31.3 reduce-scatter.1
